TPU v7x, 32 devices: a whole 2x2x4 slice. The times are simulated.
32 devices in a mesh: left: 8 (over z, x), right: 4 (over y, core).
Axes of the slice: x: 2, y: 2, z: 4, core: 2. Of those that a mesh axis runs over, the one named last changes fastest.
Arguments:
- density: float32 [128, 128, 2048], P(None, 'left', 'right'), may hold values from -6 to 6
- symbol_x: float32 [128], replicated, may hold values from 0.3 to 3
- symbol_y: float32 [128], replicated, may hold values from 0.3 to 3
- symbol_z: float32 [2048], replicated, may hold values from 0.3 to 3
Outputs:
- spectrum: float32 [128, 128, 2048], P('left', 'right')
All inputs are finite; a program needn't handle non-finite values.
Results may differ from a plain program's by a relative error of at most 0.00007.
Values sent between devices are 32-bit elements; how exact they have to be, the bound alone decides.
A program may use at most 192 MiB of HBM per device.

v0:
```python
import jax
import jax.numpy as jnp
from jax import lax
from jax.sharding import PartitionSpec as P


def mode_table(count):
    rank = jnp.arange(count)
    angle = 2.0 * jnp.pi / count * (rank[:, None] * rank[None, :] % count).astype(jnp.float32)
    return (jnp.cos(angle) + jnp.sin(angle)) * count ** (-0.5)


def transform_dim(values, dim):
    moved = jnp.tensordot(
        values, mode_table(values.shape[dim]), axes=([dim], [0]), precision=lax.Precision.HIGHEST
    )
    return jnp.moveaxis(moved, -1, dim)


def per_device(density, symbol_x, symbol_y, symbol_z):
    part_values = density
    part_values = transform_dim(part_values, 0)
    part_values = lax.all_to_all(part_values, "left", split_axis=0, concat_axis=1, tiled=True)
    part_values = transform_dim(part_values, 1)
    block_values = part_values
    block_values = lax.all_to_all(block_values, "right", split_axis=1, concat_axis=2, tiled=True)
    block_values = transform_dim(block_values, 2)
    share_x = block_values.shape[0]
    part_x = lax.dynamic_slice_in_dim(symbol_x, lax.axis_index("left") * share_x, share_x)
    share_y = block_values.shape[1]
    part_y = lax.dynamic_slice_in_dim(symbol_y, lax.axis_index("right") * share_y, share_y)
    symbol = part_x[:, None, None] + part_y[None, :, None] + symbol_z[None, None, :]
    block_values = block_values * lax.rsqrt(symbol)
    return block_values


def solution(mesh):
    return jax.shard_map(
        per_device,
        mesh=mesh,
        in_specs=(P(None, "left", "right"), P(), P(), P()),
        out_specs=P("left", "right", None),
        check_vma=False,
    )
```

profile of v0, /device:TPU:9, one launch (start us, length us, event | category | flops | bytes accessed | tf_op | source)
XLA Modules:
  0.0 244.2 jit_solution(8625823502980636644)
XLA Ops:
  0.0 9.0 %fusion.19 = f32[128,16,512]{2,0,1:T(8,128)S(1)} fusion(f32[128,16,512]{2,1,0:T(8,128)} %param.4), kind=kOutput, calls=%fused_computation.20 | convolution fusion | flops 1610874880 | bytes 8388608 | tf_op jit(solution)/shard_map/dot_general | solution.py:14
  9.0 2.4 copy.24
  11.5 96.8 %all_to_all.36 = f32[128,16,512]{2,1,0:T(8,128)S(1)} all-to-all(f32[128,16,512]{2,1,0:T(8,128)S(1)} %copy.24), channel_id=1, replica_groups=mesh['left'=8,'right'=4] {'left'}, dimensions={0} | all-to-all | bytes 8388608 | tf_op jit(solution)/shard_map/all_to_all | solution.py:23
  108.3 0.8 copy.25
  109.1 8.6 %convolution_bitcast_fusion = f32[16,128,512]{1,2,0:T(8,128)} fusion(f32[16,128,512]{2,1,0:T(8,128)S(1)} %bitcast.28), kind=kOutput, calls=%fused_computation.23 | convolution fusion | flops 1610874880 | bytes 8388608 | tf_op jit(solution)/shard_map/dot_general | solution.py:14
  117.8 5.5 %copy.27 = f32[16,128,512]{2,0,1:T(8,128)} copy(f32[16,128,512]{1,2,0:T(8,128)} %convolution_bitcast_fusion) | data formatting | bytes 8388608 | tf_op jit(solution)/shard_map/transpose | solution.py:17
  123.3 0.0 copy-start.1
  123.3 0.0 copy-start.2
  123.3 7.0 %all-to-all-start.1 = ((f32[16,128,512]{2,0,1:T(8,128)}), f32[16,128,512]{2,0,1:T(8,128)}, u32[]{:S(2)}, u32[]{:S(2)}) async-start(f32[16,128,512]{2,0,1:T(8,128)} %copy.27), calls=%async_computation.1 | async-start | bytes 8388608 | tf_op jit(solution)/shard_map/all_to_all | solution.py:26
  130.3 0.0 copy-done.1
  130.3 0.1 dynamic_slice.7
  130.4 0.0 copy-done.2
  130.4 0.1 dynamic_slice.6
  130.5 0.1 broadcast_add_fusion
  130.5 67.7 %fusion.51 = f32[2048,2048,1]{1,0,2:T(8,128)} fusion(), kind=kLoop, calls=%fused_computation.7.clone.clone.clone.1 | loop fusion | flops 67108864 | bytes 16777216 | tf_op jit(solution)/shard_map/dot_general | solution.py:14
  198.2 0.0 all-to-all-done.1
  198.2 6.9 %copy.29 = f32[16,32,4,512]{3,2,1,0:T(4,128)} copy(f32[16,32,4,512]{3,0,1,2:T(8,128)} %bitcast.8) | data formatting | bytes 8388608 | tf_op jit(solution)/shard_map/all_to_all | solution.py:26
  205.1 0.0 copy-start
  205.1 6.1 %all_to_all.33 = f32[16,32,2048]{2,1,0:T(8,128)} reshape(f32[16,32,4,512]{3,2,1,0:T(4,128)} %copy.29) | data formatting | bytes 8388608 | tf_op jit(solution)/shard_map/all_to_all | solution.py:26
  211.2 0.0 copy-done
  211.2 33.0 %rsqrt_multiply_fusion = f32[16,32,2048]{2,1,0:T(8,128)} fusion(f32[16,32,2048]{2,1,0:T(8,128)} %all_to_all.33, f32[2048]{0:T(1024)S(1)} %copy-done, f32[16,32]{1,0:T(8,128)S(1)} %broadcast_add_fusion, f32[2048,2048,1]{1,0,2:T(8,128)} %fusion.51), kind=kOutput, calls=%fused_computation.22 | convolution fusion | flops 25771900928 | bytes 25176064 | tf_op jit(solution)/shard_map/dot_general | solution.py:14
Async XLA Ops:
  123.3 7.0 %copy-start.1 = (f32[128]{0:T(128)S(1)}, f32[128]{0:T(128)}, u32[]{:S(2)}) copy-start(f32[128]{0:T(128)} %param.6) | copy-start | bytes 1540
  123.3 7.1 %copy-start.2 = (f32[128]{0:T(128)S(1)}, f32[128]{0:T(128)}, u32[]{:S(2)}) copy-start(f32[128]{0:T(128)} %param.5) | copy-start | bytes 1540
  123.3 74.9 %all-to-all-start.1 = ((f32[16,128,512]{2,0,1:T(8,128)}), f32[16,128,512]{2,0,1:T(8,128)}, u32[]{:S(2)}, u32[]{:S(2)}) async-start(f32[16,128,512]{2,0,1:T(8,128)} %copy.27), calls=%async_computation.1 | async-start | bytes 8388608 | tf_op jit(solution)/shard_map/all_to_all | solution.py:26
  205.1 6.1 %copy-start = (f32[2048]{0:T(1024)S(1)}, f32[2048]{0:T(1024)}, u32[]{:S(2)}) copy-start(f32[2048]{0:T(1024)} %param.7) | copy-start | bytes 24580
where the time goes:
time: 246 us; the launch traced here: 244 us
  blocking collectives  96.8 us (39%)
  other arithmetic  67.8 us (28%)
  matrix products  50.6 us (21%)
  local copies, waits for them, and re-layouts  21.9 us (9%)
  starting transfers between devices  7.03 us (3%)
    all_to_all x1, blocking collectives, per_device(): lax.all_to_all(part_values, 'left', split_axis=0, concat_axis=1, tiled=True)  96.8 us
    dot_general x1, other arithmetic, transform_dim(): jnp.tensordot(values, mode_table(values.shape[dim]), axes=([dim], [0]), p...  67.7 us
    dot_general x3, matrix products, transform_dim(): jnp.tensordot(values, mode_table(values.shape[dim]), axes=([dim], [0]), p...  50.6 us
    all_to_all x2, local copies, waits for them, and re-layouts, per_device(): lax.all_to_all(block_values, 'right', split_axis=1, concat_axis=2, tiled=...  13 us
    all_to_all x1, starting transfers between devices, per_device(): lax.all_to_all(block_values, 'right', split_axis=1, concat_axis=2, tiled=...  7.03 us
    transpose x1, local copies, waits for them, and re-layouts, transform_dim(): return jnp.moveaxis(moved, -1, dim)  5.51 us
  transfers between devices with their start and end apart: 1, of which 0 were waited for; matrix products, arithmetic and copies ran while one was open for 28% of the time, Pallas kernels for 0%

commit v1 on v0

v1 whole, which is shorter than its diff:
```python
import functools

import jax
import jax.numpy as jnp
import numpy as np
from jax import lax
from jax.experimental import pallas as pl
from jax.experimental.pallas import tpu as pltpu
from jax.sharding import PartitionSpec as P

LANES = 128
VMEM_BYTES = 60 * 2**20
MESH = pl.DeviceIdType.MESH
F32 = jnp.float32
BF16 = jnp.bfloat16


def mode_table(count):
    rank = jnp.arange(count)
    angle = 2.0 * jnp.pi / count * (rank[:, None] * rank[None, :] % count).astype(jnp.float32)
    return (jnp.cos(angle) + jnp.sin(angle)) * count ** (-0.5)


def transform_dim(values, dim):
    moved = jnp.tensordot(
        values, mode_table(values.shape[dim]), axes=([dim], [0]), precision=lax.Precision.HIGHEST
    )
    return jnp.moveaxis(moved, -1, dim)


def exchange_plain(density):
    values = transform_dim(density, 0)
    values = lax.all_to_all(values, "left", split_axis=0, concat_axis=1, tiled=True)
    values = transform_dim(values, 1)
    values = lax.all_to_all(values, "right", split_axis=1, concat_axis=2, tiled=True)
    return transform_dim(values, 2)


def numpy_angles(rows, count):
    return 2.0 * np.pi / count * (np.outer(rows, np.arange(count)) % count)


def two_parts(table):
    high = np.asarray(table, np.float32).astype(BF16)
    low = (table - high.astype(np.float64)).astype(np.float32).astype(BF16)
    return np.stack([high, low])


def small_table(count):
    angles = numpy_angles(np.arange(count), count)
    return two_parts((np.cos(angles) + np.sin(angles)) * count**-0.5)


def seeds(count, fine):
    coarse_angles = numpy_angles(np.arange(count // fine) * fine, count)
    coarse = np.stack([np.cos(coarse_angles), np.sin(coarse_angles)])
    fine_angles = numpy_angles(np.arange(fine), count)
    cosine, sine = np.cos(fine_angles), np.sin(fine_angles)
    return coarse.astype(np.float32), (np.stack([cosine + sine, cosine - sine]) * count**-0.5).astype(np.float32)


def split(values):
    high = values.astype(BF16)
    return high, (values - high.astype(F32)).astype(BF16)


def dot(a, b):
    return jnp.dot(a, b, preferred_element_type=F32)


def dot_three(a_high, a_low, b_high, b_low):
    return dot(a_high, b_high) + (dot(a_low, b_high) + dot(a_high, b_low))


def kernel(dims, density, table_x, table_y, coarse, fine, out, entry, send1, recv1, send2, recv2, table_high,
           table_low, part_high, part_low, total, in_sem, out_sem, s1_sem, r1_sem, s2_sem, r2_sem):
    X, Y, Z, L, R, Xl, Yl, Yr, Zl, C, zc, fine_rows = dims
    left, right = lax.axis_index("left"), lax.axis_index("right")

    def in_copy(c):
        return pltpu.make_async_copy(density.at[:, pl.ds(c * zc, zc)], entry.at[c], in_sem.at[c])

    for c in range(C):
        in_copy(c).start()

    def partner(index, step, count):
        if count & (count - 1) == 0:
            return index ^ step
        return lax.rem(index + step, count)

    def source(index, step, count):
        if count & (count - 1) == 0:
            return index ^ step
        return lax.rem(index + count - step, count)

    barrier = pltpu.get_barrier_semaphore()
    for step in range(1, L):
        pl.semaphore_signal(barrier, inc=1, device_id=(partner(left, step, L), right), device_id_type=MESH)
    for step in range(1, R):
        pl.semaphore_signal(barrier, inc=1, device_id=(left, partner(right, step, R)), device_id_type=MESH)
    pl.semaphore_wait(barrier, L + R - 2)

    def copy1(c, step):
        to = partner(left, step, L)
        return pltpu.make_async_remote_copy(
            src_ref=send1.at[c, pl.ds(to * Xl, Xl)],
            dst_ref=recv1.at[c, :, pl.ds(pl.multiple_of(left * Yl, 8), Yl), :],
            send_sem=s1_sem.at[c, step],
            recv_sem=r1_sem.at[c, step],
            device_id=(to, right),
            device_id_type=MESH,
        )

    def copy2(c, step):
        to = partner(right, step, R)
        return pltpu.make_async_remote_copy(
            src_ref=send2.at[c, :, pl.ds(pl.multiple_of(to * Yr, 8), Yr), :],
            dst_ref=recv2.at[c, :, :, pl.ds(pl.multiple_of(right * zc, LANES), zc)],
            send_sem=s2_sem.at[c, step],
            recv_sem=r2_sem.at[c, step],
            device_id=(left, to),
            device_id_type=MESH,
        )

    group = 4

    def first(c):
        in_copy(c).wait()
        high, low = table_x[0], table_x[1]
        target = send1.at[c].reshape(X * Yl, zc)

        def body(g, _):
            lines = [entry[c, pl.ds(g * group + j, X, stride=Yl), :] for j in range(group)]
            b_high, b_low = split(jnp.concatenate(lines, axis=1))
            moved = dot_three(high, low, b_high, b_low)
            for j in range(group):
                target[pl.ds(g * group + j, X, stride=Yl), :] = moved[:, j * zc:(j + 1) * zc]
            return 0

        lax.fori_loop(0, Yl // group, body, 0)
        for step in range(1, L):
            copy1(c, step).start()
        recv1[c, :, pl.ds(pl.multiple_of(left * Yl, 8), Yl), :] = send1[c, pl.ds(left * Xl, Xl)]

    def second(c):
        for step in range(1, L):
            copy1(c, step).wait_recv()
        high, low = table_y[0], table_y[1]

        def body(g, _):
            lines = [recv1[c, g * group + j] for j in range(group)]
            b_high, b_low = split(jnp.concatenate(lines, axis=1))
            moved = dot_three(high, low, b_high, b_low)
            for j in range(group):
                send2[c, g * group + j] = moved[:, j * zc:(j + 1) * zc]
            return 0

        lax.fori_loop(0, Xl // group, body, 0)
        for step in range(1, R):
            copy2(c, step).start()
        recv2[c, :, :, pl.ds(pl.multiple_of(right * zc, LANES), zc)] = send2[
            c, :, pl.ds(pl.multiple_of(right * Yr, 8), Yr), :]

    rows = Xl * Yr
    wide = 512

    def third(c):
        for step in range(1, R):
            copy2(c, step).wait_recv()

        def split_body(x, _):
            high, low = split(recv2[c, x])
            at = pl.ds(pl.multiple_of(x * Yr, 16), Yr)
            part_high[at, :] = high
            part_low[at, :] = low
            return 0

        lax.fori_loop(0, Xl, split_body, 0)

        def body(n, _):
            at = pl.ds(pl.multiple_of(n * wide, LANES), wide)
            term = dot_three(part_high[...], part_low[...], table_high[c, :, at], table_low[c, :, at])
            if c > 0:
                term = total[:, at] + term
            total[:, at] = term
            if c == C - 1:
                pltpu.make_async_copy(total.at[:, at], out.at[:, at], out_sem.at[n]).start()
            return 0

        lax.fori_loop(0, Z // wide, body, 0)

    def tables(c):
        per = zc // fine_rows

        def body(i, _):
            base = lax.div(i, per) * (Zl // fine_rows) + c * per + lax.rem(i, per)
            cosine, sine = coarse[0, pl.ds(base, 1), :], coarse[1, pl.ds(base, 1), :]

            def inner(q, _):
                at = pl.ds(pl.multiple_of(q * 16, 16), 16)
                high, low = split(cosine * fine[0, at, :] + sine * fine[1, at, :])
                to = pl.ds(pl.multiple_of(i * fine_rows + q * 16, 16), 16)
                table_high[c, to, :] = high
                table_low[c, to, :] = low
                return 0

            return lax.fori_loop(0, fine_rows // 16, inner, 0)

        lax.fori_loop(0, R * per, body, 0)

    for c in range(C):
        first(c)
    for c in range(C):
        tables(c)
    for c in range(C):
        second(c)
        if c > 0:
            third(c - 1)
    third(C - 1)

    for n in range(Z // wide):
        at = pl.ds(n * wide, wide)
        pltpu.make_async_copy(total.at[:, at], out.at[:, at], out_sem.at[n]).wait()
    for c in range(C):
        for step in range(1, L):
            copy1(c, step).wait_send()
        for step in range(1, R):
            copy2(c, step).wait_send()


def exchange_kernel(density, L, R, fine_rows, Z):
    X, Yl, Zl = density.shape
    Y, Xl = Yl * L, X // L
    Yr, zc = Y // R, LANES
    C = Zl // zc
    dims = (X, Y, Z, L, R, Xl, Yl, Yr, Zl, C, zc, fine_rows)
    coarse, fine = seeds(Z, fine_rows)
    vmem = pl.BlockSpec(memory_space=pltpu.VMEM)
    hbm = pl.BlockSpec(memory_space=pl.ANY)
    dma = pltpu.SemaphoreType.DMA
    flat = pl.pallas_call(
        functools.partial(kernel, dims),
        out_shape=jax.ShapeDtypeStruct((Xl * Yr, Z), F32),
        in_specs=[hbm, vmem, vmem, vmem, vmem],
        out_specs=hbm,
        scratch_shapes=[
            pltpu.VMEM((C, X * Yl, zc), F32),
            pltpu.VMEM((C, X, Yl, zc), F32),
            pltpu.VMEM((C, Xl, Y, zc), F32),
            pltpu.VMEM((C, Xl, Y, zc), F32),
            pltpu.VMEM((C, Xl, Yr, R * zc), F32),
            pltpu.VMEM((C, R * zc, Z), BF16),
            pltpu.VMEM((C, R * zc, Z), BF16),
            pltpu.VMEM((Xl * Yr, R * zc), BF16),
            pltpu.VMEM((Xl * Yr, R * zc), BF16),
            pltpu.VMEM((Xl * Yr, Z), F32),
            dma((C,)),
            dma((Z // 512,)),
            dma((C, L)),
            dma((C, L)),
            dma((C, R)),
            dma((C, R)),
        ],
        compiler_params=pltpu.CompilerParams(
            collective_id=0, has_side_effects=True, vmem_limit_bytes=VMEM_BYTES
        ),
    )(density.reshape(X * Yl, Zl), small_table(X), small_table(Y), coarse, fine)
    return flat.reshape(Xl, Yr, Z)


def per_device(L, R, density, symbol_x, symbol_y, symbol_z):
    X, Yl, Zl = density.shape
    Z = Zl * R
    fine_rows = 64
    held = 6 * density.size * 4 + 2 * Z * Z * 2 + 2 * (Z // fine_rows + fine_rows) * Z * 4 + 8 * 2**20
    fits = (held <= VMEM_BYTES and Zl % LANES == 0 and Z % 512 == 0 and Yl % 8 == 0 and X % (4 * L) == 0
            and Yl * L % (16 * R) == 0)
    block_values = exchange_kernel(density, L, R, fine_rows, Z) if fits else exchange_plain(density)
    share_x = block_values.shape[0]
    part_x = lax.dynamic_slice_in_dim(symbol_x, lax.axis_index("left") * share_x, share_x)
    share_y = block_values.shape[1]
    part_y = lax.dynamic_slice_in_dim(symbol_y, lax.axis_index("right") * share_y, share_y)
    symbol = part_x[:, None, None] + part_y[None, :, None] + symbol_z[None, None, :]
    return block_values * lax.rsqrt(symbol)


def solution(mesh):
    return jax.shard_map(
        functools.partial(per_device, mesh.shape["left"], mesh.shape["right"]),
        mesh=mesh,
        in_specs=(P(None, "left", "right"), P(), P(), P()),
        out_specs=P("left", "right", None),
        check_vma=False,
    )
```

time: 246 us -> 124 us (0.50)
  Pallas kernels: 0 us -> 117 us
  blocking collectives: 96.8 us -> 0 us
  other arithmetic: 67.8 us -> 4.91 us
  matrix products: 50.6 us -> 0 us
  local copies, waits for them, and re-layouts: 21.9 us -> 1.46 us
  starting transfers between devices: 7.03 us -> 0 us
    pallas_call x0 -> x1, Pallas kernels: none -> 117 us  [exchange_kernel(): pl.pallas_call(functools.partial(kernel, dims), out_shape=jax.ShapeDtypeS...]
    all_to_all x1 -> x0, blocking collectives: 96.8 us -> none  [per_device(): lax.all_to_all(part_values, 'left', split_axis=0, concat_axis=1, tiled=True)]
    dot_general x1 -> x0, other arithmetic: 67.7 us -> none  [transform_dim(): jnp.tensordot(values, mode_table(values.shape[dim]), axes=([dim], [0]), p...]
    dot_general x3 -> x0, matrix products: 50.6 us -> none  [transform_dim(): jnp.tensordot(values, mode_table(values.shape[dim]), axes=([dim], [0]), p...]
    all_to_all x3 -> x0, local copies, waits for them, and re-layouts: 13.8 us -> none  [the longest x2 13 us: per_device(): lax.all_to_all(block_values, 'right', split_axis=1, concat_axis=2, tiled=...]
    all_to_all x1 -> x0, starting transfers between devices: 7.03 us -> none  [per_device(): lax.all_to_all(block_values, 'right', split_axis=1, concat_axis=2, tiled=...]
    transpose x1 -> x0, local copies, waits for them, and re-layouts: 5.51 us -> none  [transform_dim(): return jnp.moveaxis(moved, -1, dim)]
    mul x0 -> x1, other arithmetic: none -> 4.84 us  [per_device(): return block_values * lax.rsqrt(symbol)]
  transfers between devices with their start and end apart: 1 -> 0, of which waited for: 0 -> 0; matrix products, arithmetic and copies ran while one was open for 28% -> 0% of each run, Pallas kernels for 0% -> 0%
where the time goes in v1:
time: 124 us
  Pallas kernels  117 us (94%)
  other arithmetic  4.91 us (4%)
  local copies, waits for them, and re-layouts  1.46 us (1%)
    pallas_call x1, Pallas kernels, exchange_kernel(): pl.pallas_call(functools.partial(kernel, dims), out_shape=jax.ShapeDtypeS...  117 us
    mul x1, other arithmetic, per_device(): return block_values * lax.rsqrt(symbol)  4.84 us

profile of v1, /device:TPU:9, one launch (start us, length us, event | category | flops | bytes accessed | tf_op | source)
XLA Modules:
  0.0 123.7 jit_solution(17111160577587407048)
XLA Ops:
  0.0 0.7 dynamic_slice.7
  0.7 0.7 dynamic_slice.6
  1.5 0.1 broadcast_add_fusion
  1.5 0.0 copy-start
  1.5 117.3 %shard_map.82 = f32[512,2048]{1,0:T(8,128)} custom-call(f32[2048,512]{1,0:T(8,128)} %bitcast.3, bf16[2,128,128]{2,1,0:T(8,128)(2,1)} %constant.23.clone.table_x.table_y, bf16[2,128,128]{2,1,0:T(8,128)(2,1)} %constant.23.clone.table_x.table_y, f32[2,32,2048]{2,1,0:T(8,128)} %constant.24.clone.coarse, f32[2,64,2048]{2,1,0:T(8,128)} %constant.25.clone.fine), custom_call_target="tpu_custom_call" | custom-call | tf_op jit(solution)/shard_map/pallas_call | solution.py:241
  118.8 0.0 copy-done
  118.8 4.8 %rsqrt_multiply_fusion = f32[16,32,2048]{2,1,0:T(8,128)} fusion(f32[16,32,2048]{2,1,0:T(8,128)} %bitcast.2, f32[2048]{0:T(1024)S(1)} %copy-done, f32[16,32]{1,0:T(8,128)S(1)} %broadcast_add_fusion), kind=kLoop, calls=%fused_computation | loop fusion | flops 2097152 | bytes 8398848 | tf_op jit(solution)/shard_map/mul | solution.py:284
Async XLA Ops:
  1.5 117.3 %copy-start = (f32[2048]{0:T(1024)S(1)}, f32[2048]{0:T(1024)}, u32[]{:S(2)}) copy-start(f32[2048]{0:T(1024)} %param.11) | copy-start | bytes 24580

commit v2 on v1

--- a/solution.py
+++ b/solution.py
@@ -72,57 +72,61 @@
     return dot(a_high, b_high) + (dot(a_low, b_high) + dot(a_high, b_low))
 
 
-def kernel(dims, density, table_x, table_y, coarse, fine, out, entry, send1, recv1, send2, recv2, table_high,
-           table_low, part_high, part_low, total, in_sem, out_sem, s1_sem, r1_sem, s2_sem, r2_sem):
+def kernel(dims, parts, density, table_x, table_y, coarse_in, fine_in, symbol_x, symbol_y, symbol_z, out, entry,
+           send1, recv1, send2, recv2, table_high, table_low, part_high, part_low, total, scale, coarse, fine,
+           in_sem, seed_sem, out_sem, s1_sem, r1_sem, s2_sem, r2_sem):
     X, Y, Z, L, R, Xl, Yl, Yr, Zl, C, zc, fine_rows = dims
     left, right = lax.axis_index("left"), lax.axis_index("right")
 
     def in_copy(c):
         return pltpu.make_async_copy(density.at[:, pl.ds(c * zc, zc)], entry.at[c], in_sem.at[c])
 
-    for c in range(C):
-        in_copy(c).start()
+    seed_copies = [
+        pltpu.make_async_copy(coarse_in, coarse, seed_sem.at[0]),
+        pltpu.make_async_copy(fine_in, fine, seed_sem.at[1]),
+    ]
 
     def partner(index, step, count):
         if count & (count - 1) == 0:
             return index ^ step
         return lax.rem(index + step, count)
-
-    def source(index, step, count):
-        if count & (count - 1) == 0:
-            return index ^ step
-        return lax.rem(index + count - step, count)
 
     barrier = pltpu.get_barrier_semaphore()
     for step in range(1, L):
         pl.semaphore_signal(barrier, inc=1, device_id=(partner(left, step, L), right), device_id_type=MESH)
     for step in range(1, R):
         pl.semaphore_signal(barrier, inc=1, device_id=(left, partner(right, step, R)), device_id_type=MESH)
-    pl.semaphore_wait(barrier, L + R - 2)
-
-    def copy1(c, step):
+    for c in range(C):
+        in_copy(c).start()
+    for copy in seed_copies:
+        copy.start()
+
+    def copy1(p, step):
+        c, x0, xn = parts[p]
         to = partner(left, step, L)
         return pltpu.make_async_remote_copy(
-            src_ref=send1.at[c, pl.ds(to * Xl, Xl)],
-            dst_ref=recv1.at[c, :, pl.ds(pl.multiple_of(left * Yl, 8), Yl), :],
-            send_sem=s1_sem.at[c, step],
-            recv_sem=r1_sem.at[c, step],
+            src_ref=send1.at[c, pl.ds(to * Xl + x0, xn)],
+            dst_ref=recv1.at[c, pl.ds(x0, xn), pl.ds(pl.multiple_of(left * Yl, 8), Yl), :],
+            send_sem=s1_sem.at[p, step],
+            recv_sem=r1_sem.at[p, step],
             device_id=(to, right),
             device_id_type=MESH,
         )
 
-    def copy2(c, step):
+    def copy2(p, step):
+        c, x0, xn = parts[p]
         to = partner(right, step, R)
         return pltpu.make_async_remote_copy(
-            src_ref=send2.at[c, :, pl.ds(pl.multiple_of(to * Yr, 8), Yr), :],
-            dst_ref=recv2.at[c, :, :, pl.ds(pl.multiple_of(right * zc, LANES), zc)],
-            send_sem=s2_sem.at[c, step],
-            recv_sem=r2_sem.at[c, step],
+            src_ref=send2.at[c, pl.ds(x0, xn), pl.ds(pl.multiple_of(to * Yr, 8), Yr), :],
+            dst_ref=recv2.at[c, pl.ds(x0, xn), :, pl.ds(pl.multiple_of(right * zc, LANES), zc)],
+            send_sem=s2_sem.at[p, step],
+            recv_sem=r2_sem.at[p, step],
             device_id=(left, to),
             device_id_type=MESH,
         )
 
     group = 4
+    wide = 512
 
     def first(c):
         in_copy(c).wait()
@@ -138,35 +142,45 @@
             return 0
 
         lax.fori_loop(0, Yl // group, body, 0)
+
+    def first_send(c):
+        for p, part in enumerate(parts):
+            if part[0] == c:
+                for step in range(1, L):
+                    copy1(p, step).start()
+        recv1[c, :, pl.ds(pl.multiple_of(left * Yl, 8), Yl), :] = send1[c, pl.ds(left * Xl, Xl)]
+
+    def second(p):
+        c, x0, xn = parts[p]
         for step in range(1, L):
-            copy1(c, step).start()
-        recv1[c, :, pl.ds(pl.multiple_of(left * Yl, 8), Yl), :] = send1[c, pl.ds(left * Xl, Xl)]
-
-    def second(c):
-        for step in range(1, L):
-            copy1(c, step).wait_recv()
+            copy1(p, step).wait_recv()
         high, low = table_y[0], table_y[1]
+        lot = min(group, xn)
 
         def body(g, _):
-            lines = [recv1[c, g * group + j] for j in range(group)]
+            x = x0 + g * lot
+            lines = [recv1[c, x + j] for j in range(lot)]
             b_high, b_low = split(jnp.concatenate(lines, axis=1))
             moved = dot_three(high, low, b_high, b_low)
-            for j in range(group):
-                send2[c, g * group + j] = moved[:, j * zc:(j + 1) * zc]
-            return 0
-
-        lax.fori_loop(0, Xl // group, body, 0)
+            for j in range(lot):
+                send2[c, x + j] = moved[:, j * zc:(j + 1) * zc]
+            return 0
+
+        lax.fori_loop(0, xn // lot, body, 0)
         for step in range(1, R):
-            copy2(c, step).start()
-        recv2[c, :, :, pl.ds(pl.multiple_of(right * zc, LANES), zc)] = send2[
-            c, :, pl.ds(pl.multiple_of(right * Yr, 8), Yr), :]
-
-    rows = Xl * Yr
-    wide = 512
-
-    def third(c):
+            copy2(p, step).start()
+        recv2[c, pl.ds(x0, xn), :, pl.ds(pl.multiple_of(right * zc, LANES), zc)] = send2[
+            c, pl.ds(x0, xn), pl.ds(pl.multiple_of(right * Yr, 8), Yr), :]
+
+    def out_copy(p, n):
+        c, x0, xn = parts[p]
+        rows, at = pl.ds(x0 * Yr, xn * Yr), pl.ds(pl.multiple_of(n * wide, LANES), wide)
+        return pltpu.make_async_copy(total.at[rows, at], out.at[rows, at], out_sem.at[p, n])
+
+    def third(p):
+        c, x0, xn = parts[p]
         for step in range(1, R):
-            copy2(c, step).wait_recv()
+            copy2(p, step).wait_recv()
 
         def split_body(x, _):
             high, low = split(recv2[c, x])
@@ -175,16 +189,19 @@
             part_low[at, :] = low
             return 0
 
-        lax.fori_loop(0, Xl, split_body, 0)
+        lax.fori_loop(x0, x0 + xn, split_body, 0)
+        rows = pl.ds(x0 * Yr, xn * Yr)
 
         def body(n, _):
             at = pl.ds(pl.multiple_of(n * wide, LANES), wide)
-            term = dot_three(part_high[...], part_low[...], table_high[c, :, at], table_low[c, :, at])
+            term = dot_three(part_high[rows, :], part_low[rows, :], table_high[c, :, at], table_low[c, :, at])
             if c > 0:
-                term = total[:, at] + term
-            total[:, at] = term
+                term = total[rows, at] + term
             if c == C - 1:
-                pltpu.make_async_copy(total.at[:, at], out.at[:, at], out_sem.at[n]).start()
+                term = term * scale[rows, at]
+            total[rows, at] = term
+            if c == C - 1:
+                out_copy(p, n).start()
             return 0
 
         lax.fori_loop(0, Z // wide, body, 0)
@@ -208,40 +225,69 @@
 
         lax.fori_loop(0, R * per, body, 0)
 
-    for c in range(C):
+    def scales():
+        line = lax.broadcasted_iota(jnp.int32, (Yr, LANES), 0)
+        column = jnp.zeros((Yr, LANES), F32)
+        for j in range(Yr):
+            column = jnp.where(line == j, symbol_y[right * Yr + j], column)
+
+        def body(x, _):
+            start = column + symbol_x[left * Xl + x]
+            rows = pl.ds(pl.multiple_of(x * Yr, 8), Yr)
+            for k in range(0, Z, LANES):
+                scale[rows, k:k + LANES] = lax.rsqrt(start + symbol_z[:, k:k + LANES])
+            return 0
+
+        lax.fori_loop(0, Xl, body, 0)
+
+    first(0)
+    pl.semaphore_wait(barrier, L + R - 2)
+    first_send(0)
+    for c in range(1, C):
         first(c)
+        first_send(c)
+    for copy in seed_copies:
+        copy.wait()
     for c in range(C):
         tables(c)
-    for c in range(C):
-        second(c)
-        if c > 0:
-            third(c - 1)
-    third(C - 1)
-
-    for n in range(Z // wide):
-        at = pl.ds(n * wide, wide)
-        pltpu.make_async_copy(total.at[:, at], out.at[:, at], out_sem.at[n]).wait()
-    for c in range(C):
+    scales()
+    for p in range(len(parts)):
+        second(p)
+        if p > 0:
+            third(p - 1)
+    third(len(parts) - 1)
+
+    for p, part in enumerate(parts):
+        if part[0] == C - 1:
+            for n in range(Z // wide):
+                out_copy(p, n).wait()
+    for p in range(len(parts)):
         for step in range(1, L):
-            copy1(c, step).wait_send()
+            copy1(p, step).wait_send()
         for step in range(1, R):
-            copy2(c, step).wait_send()
-
-
-def exchange_kernel(density, L, R, fine_rows, Z):
+            copy2(p, step).wait_send()
+
+
+CUTS = (1, 2, 2, 4)
+
+
+def exchange_kernel(density, symbol_x, symbol_y, symbol_z, L, R, fine_rows):
     X, Yl, Zl = density.shape
-    Y, Xl = Yl * L, X // L
+    Y, Xl, Z = Yl * L, X // L, Zl * R
     Yr, zc = Y // R, LANES
     C = Zl // zc
     dims = (X, Y, Z, L, R, Xl, Yl, Yr, Zl, C, zc, fine_rows)
+    cuts = [1] * (C - len(CUTS)) + list(CUTS[-C:])
+    parts = [(c, i * (Xl // cuts[c]), Xl // cuts[c]) for c in range(C) for i in range(cuts[c])]
     coarse, fine = seeds(Z, fine_rows)
     vmem = pl.BlockSpec(memory_space=pltpu.VMEM)
+    smem = pl.BlockSpec(memory_space=pltpu.SMEM)
     hbm = pl.BlockSpec(memory_space=pl.ANY)
     dma = pltpu.SemaphoreType.DMA
     flat = pl.pallas_call(
-        functools.partial(kernel, dims),
+        functools.partial(kernel, dims, parts),
         out_shape=jax.ShapeDtypeStruct((Xl * Yr, Z), F32),
-        in_specs=[hbm, vmem, vmem, vmem, vmem],
+        in_specs=[hbm, vmem, vmem, hbm, hbm, smem, smem, vmem],
         out_specs=hbm,
         scratch_shapes=[
             pltpu.VMEM((C, X * Yl, zc), F32),
@@ -254,17 +300,22 @@
             pltpu.VMEM((Xl * Yr, R * zc), BF16),
             pltpu.VMEM((Xl * Yr, R * zc), BF16),
             pltpu.VMEM((Xl * Yr, Z), F32),
+            pltpu.VMEM((Xl * Yr, Z), F32),
+            pltpu.VMEM(coarse.shape, F32),
+            pltpu.VMEM(fine.shape, F32),
             dma((C,)),
-            dma((Z // 512,)),
-            dma((C, L)),
-            dma((C, L)),
-            dma((C, R)),
-            dma((C, R)),
+            dma((2,)),
+            dma((len(parts), Z // 512)),
+            dma((len(parts), L)),
+            dma((len(parts), L)),
+            dma((len(parts), R)),
+            dma((len(parts), R)),
         ],
         compiler_params=pltpu.CompilerParams(
             collective_id=0, has_side_effects=True, vmem_limit_bytes=VMEM_BYTES
         ),
-    )(density.reshape(X * Yl, Zl), small_table(X), small_table(Y), coarse, fine)
+    )(density.reshape(X * Yl, Zl), small_table(X), small_table(Y), coarse, fine, symbol_x, symbol_y,
+      symbol_z.reshape(1, Z))
     return flat.reshape(Xl, Yr, Z)
 
 
@@ -272,10 +323,12 @@
     X, Yl, Zl = density.shape
     Z = Zl * R
     fine_rows = 64
-    held = 6 * density.size * 4 + 2 * Z * Z * 2 + 2 * (Z // fine_rows + fine_rows) * Z * 4 + 8 * 2**20
-    fits = (held <= VMEM_BYTES and Zl % LANES == 0 and Z % 512 == 0 and Yl % 8 == 0 and X % (4 * L) == 0
+    held = 7 * density.size * 4 + 2 * Z * Z * 2 + 2 * (Z // fine_rows + fine_rows) * Z * 4 + 4 * 2**20
+    fits = (held <= VMEM_BYTES and Zl % LANES == 0 and Z % 512 == 0 and Yl % 8 == 0 and X % (16 * L) == 0
             and Yl * L % (16 * R) == 0)
-    block_values = exchange_kernel(density, L, R, fine_rows, Z) if fits else exchange_plain(density)
+    if fits:
+        return exchange_kernel(density, symbol_x, symbol_y, symbol_z, L, R, fine_rows)
+    block_values = exchange_plain(density)
     share_x = block_values.shape[0]
     part_x = lax.dynamic_slice_in_dim(symbol_x, lax.axis_index("left") * share_x, share_x)
     share_y = block_values.shape[1]

time: 124 us -> 117 us (0.944)
  Pallas kernels: 117 us -> 112 us
  other arithmetic: 4.91 us -> 0 us
  local copies, waits for them, and re-layouts: 1.46 us -> 4.7 us
    pallas_call x1, Pallas kernels: 117 us -> 112 us  [exchange_kernel(): pl.pallas_call(functools.partial(kernel, dims, parts), out_shape=jax.Shap...]
    mul x1 -> x0, other arithmetic: 4.84 us -> none  [per_device(): return block_values * lax.rsqrt(symbol)]
    unnamed x2 -> x1, local copies, waits for them, and re-layouts: 0.01 us -> 4.7 us
    dynamic_slice x2 -> x0, local copies, waits for them, and re-layouts: 1.45 us -> none  [the longest x1 0.73 us: per_device(): lax.dynamic_slice_in_dim(symbol_x, lax.axis_index('left') * share_x, shar...]
where the time goes in v2:
time: 117 us
  Pallas kernels  112 us (96%)
  local copies, waits for them, and re-layouts  4.7 us (4%)
    pallas_call x1, Pallas kernels, exchange_kernel(): pl.pallas_call(functools.partial(kernel, dims, parts), out_shape=jax.Shap...  112 us
    unnamed x1, local copies, waits for them, and re-layouts  4.7 us

profile of v2, /device:TPU:9, one launch (start us, length us, event | category | flops | bytes accessed | tf_op | source)
XLA Modules:
  0.0 116.8 jit_solution(13776820705450237023)
XLA Ops:
  0.0 112.1 %shard_map.82 = f32[512,2048]{1,0:T(8,128)} custom-call(f32[2048,512]{1,0:T(8,128)} %bitcast.4, bf16[2,128,128]{2,1,0:T(8,128)(2,1)} %constant.6.clone.table_x.table_y, bf16[2,128,128]{2,1,0:T(8,128)(2,1)} %constant.6.clone.table_x.table_y, f32[2,32,2048]{2,1,0:T(8,128)} %constant.7.clone.coarse_in, f32[2,64,2048]{2,1,0:T(8,128)} %constant.8.clone.fine_in, ...), custom_call_target="tpu_custom_call" | custom-call | tf_op jit(solution)/shard_map/pallas_call | solution.py:287
  112.1 4.7 %copy.10 = f32[16,32,2048]{2,1,0:T(8,128)} copy(f32[16,32,2048]{2,1,0:T(8,128)} %bitcast.3) | data formatting | bytes 8388608

commit v3 on v2

--- a/solution.py
+++ b/solution.py
@@ -251,11 +251,14 @@
     for c in range(C):
         tables(c)
     scales()
-    for p in range(len(parts)):
+    done = 0
+    for p, part in enumerate(parts):
         second(p)
-        if p > 0:
-            third(p - 1)
-    third(len(parts) - 1)
+        if part[0] < C - 1 and p > 0:
+            third(done)
+            done += 1
+    for p in range(done, len(parts)):
+        third(p)
 
     for p, part in enumerate(parts):
         if part[0] == C - 1:

time: 117 us -> 116 us (level); the launches traced: 117 us -> 114 us
  Pallas kernels: 112 us -> 110 us
    pallas_call x1, Pallas kernels: 112 us -> 110 us  [exchange_kernel(): pl.pallas_call(functools.partial(kernel, dims, parts), out_shape=jax.Shap...]
where the time goes in v3:
time: 116 us; the launch traced here: 114 us
  Pallas kernels  110 us (95%)
  local copies, waits for them, and re-layouts  4.7 us (4%)
    pallas_call x1, Pallas kernels, exchange_kernel(): pl.pallas_call(functools.partial(kernel, dims, parts), out_shape=jax.Shap...  110 us
    unnamed x1, local copies, waits for them, and re-layouts  4.7 us

profile of v3, /device:TPU:9, one launch (start us, length us, event | category | flops | bytes accessed | tf_op | source)
XLA Modules:
  0.0 114.2 jit_solution(13345918909394051246)
XLA Ops:
  0.0 109.5 %shard_map.82 = f32[512,2048]{1,0:T(8,128)} custom-call(f32[2048,512]{1,0:T(8,128)} %bitcast.4, bf16[2,128,128]{2,1,0:T(8,128)(2,1)} %constant.6.clone.table_x.table_y, bf16[2,128,128]{2,1,0:T(8,128)(2,1)} %constant.6.clone.table_x.table_y, f32[2,32,2048]{2,1,0:T(8,128)} %constant.7.clone.coarse_in, f32[2,64,2048]{2,1,0:T(8,128)} %constant.8.clone.fine_in, ...), custom_call_target="tpu_custom_call" | custom-call | tf_op jit(solution)/shard_map/pallas_call | solution.py:290
  109.5 4.7 %copy.10 = f32[16,32,2048]{2,1,0:T(8,128)} copy(f32[16,32,2048]{2,1,0:T(8,128)} %bitcast.3) | data formatting | bytes 8388608
